TPU v7x, 32 devices: a whole 2x2x4 slice. The times are simulated.
32 devices in a mesh: site: 16 (over z, x, core), sec: 2 (over y).
Axes of the slice: x: 2, y: 2, z: 4, core: 2. Of those that a mesh axis runs over, the one named last changes fastest.
Arguments:
- left_canon: bfloat16 [16, 4, 4, 128, 128], P('site', None, 'sec'), may hold values from -1.5 to 1.5
- right_canon: bfloat16 [16, 4, 4, 128, 128], P('site', None, 'sec'), may hold values from -1.5 to 1.5
- center_site: bfloat16 [16, 4, 4, 128, 128], P('site', None, 'sec'), may hold values from -6 to 6
- center_bond: bfloat16 [16, 4, 128, 128], P('site', 'sec'), may hold values from -2 to 3
- left_seed: bfloat16 [16, 4, 128, 128], P('site', 'sec'), may hold values from -2 to 4
- right_seed: bfloat16 [16, 4, 128, 128], P('site', 'sec'), may hold values from -2 to 4
- left_sector: int32 [16, 4, 4], P('site'), may hold values from 0 to 3, each once within a row
- onsite: float32 [16, 4], P('site'), may hold values from 0.5 to 2
- bond_shift: float32 [16], P('site'), may hold values from 0.5 to 2
Outputs:
- left_new: bfloat16 [16, 4, 4, 128, 128], P('site', None, 'sec')
- right_new: bfloat16 [16, 4, 4, 128, 128], P('site', None, 'sec')
Inputs may be any that keep to these rules, and one draw needn't show every extreme that they name: `left_sector`: for each site and local state the 4 entries are a permutation of the sectors.
All inputs are finite; a program needn't handle non-finite values.
Results may differ from a plain program's by a relative error of at most 0.028.
Values may be sent and summed in bfloat16 or wider, within the bound.
A program may use at most 64 MiB of HBM per device.

v0:
```python
import jax
import jax.numpy as jnp
from jax import lax
from jax.sharding import PartitionSpec as P

NSI = 10
NAPP = 2


def from_behind(block, axis, distance):
    devices = range(lax.axis_size(axis))
    route = [((i - distance) % len(devices), i) for i in devices]
    return lax.ppermute(block, axis, route)


def inverse_root(gram_mat):
    scaling = jnp.sqrt(jnp.sum(gram_mat * gram_mat, axis=(-2, -1), keepdims=True))
    identity = jnp.eye(gram_mat.shape[-1], dtype=jnp.float32)
    upper_part = gram_mat / scaling
    lower_part = jnp.broadcast_to(identity, gram_mat.shape)
    for repeat in range(NSI):
        middle = 1.5 * identity - 0.5 * jnp.matmul(
            lower_part, upper_part, precision=lax.Precision.HIGHEST
        )
        upper_part = jnp.matmul(upper_part, middle, precision=lax.Precision.HIGHEST)
        lower_part = jnp.matmul(middle, lower_part, precision=lax.Precision.HIGHEST)
    return lower_part / jnp.sqrt(scaling)


def trace_sum(blocks):
    return jnp.sum(jnp.diagonal(blocks.astype(jnp.float32), axis1=1, axis2=2))


def left_turn(hold_full, tensor_blocks, indices):
    running = jnp.zeros(tensor_blocks.shape[1:], jnp.float32)
    for physical in range(tensor_blocks.shape[0]):
        chosen = jnp.take(hold_full, indices[physical], axis=0)
        product = jnp.einsum(
            "kab,kbc->kac", chosen, tensor_blocks[physical], preferred_element_type=jnp.float32
        ).astype(jnp.bfloat16)
        running = running + jnp.einsum(
            "kba,kbc->kac", tensor_blocks[physical], product, preferred_element_type=jnp.float32
        )
    return running.astype(jnp.bfloat16)


def right_turn(hold_full, tensor_all, indices):
    running = jnp.zeros((indices.shape[1],) + hold_full.shape[1:], jnp.float32)
    for physical in range(tensor_all.shape[0]):
        picked = jnp.take(tensor_all[physical], indices[physical], axis=0)
        env_chosen = jnp.take(hold_full, indices[physical], axis=0)
        product = jnp.einsum(
            "kab,kbc->kac", picked, env_chosen, preferred_element_type=jnp.float32
        ).astype(jnp.bfloat16)
        running = running + jnp.einsum(
            "kac,kdc->kad", product, picked, preferred_element_type=jnp.float32
        )
    return running.astype(jnp.bfloat16)


def right_polar(gram_right, previous):
    gram_prev = jnp.einsum("kab,kcb->kac", previous, previous, preferred_element_type=jnp.float32)
    unit_right = jnp.matmul(
        inverse_root(gram_prev), previous.astype(jnp.float32), precision=lax.Precision.HIGHEST
    )
    return jnp.matmul(
        jnp.swapaxes(unit_right, -1, -2), inverse_root(gram_right), precision=lax.Precision.HIGHEST
    ).astype(jnp.bfloat16)


def per_device(
    left_canon,
    right_canon,
    center_site,
    center_bond,
    left_seed,
    right_seed,
    left_sector,
    onsite,
    bond_shift,
):
    canon_left = left_canon[0]
    canon_right = right_canon[0]
    site_now = center_site[0]
    bond_now = center_bond[0]
    sources = left_sector[0]
    energy = onsite[0]
    bond_add = bond_shift[0]
    owned = canon_left.shape[1]
    width = canon_left.shape[2]
    sectors = sources.shape[1]
    offset = lax.axis_index("sec") * owned
    labels = jnp.arange(sectors, dtype=jnp.int32)
    right_of = jnp.sum(
        jnp.where(sources[:, :, None] == labels[None, None, :], labels[None, :, None], 0), axis=1
    )
    own_sources = lax.dynamic_slice_in_dim(sources, offset, owned, 1)
    steps_total = lax.axis_size("site") // 4
    dim_all = sectors * width
    all_left, all_right, left_start, right_start = (
        lax.all_gather(canon_left, "sec", axis=1, tiled=True),
        lax.all_gather(canon_right, "sec", axis=1, tiled=True),
        lax.all_gather(left_seed[0], "sec", axis=0, tiled=True),
        lax.all_gather(right_seed[0], "sec", axis=0, tiled=True),
    )

    def chain_turn(count_now, state_tuple):
        left_hold, right_hold, left_last = state_tuple
        left_fresh = left_turn(left_hold, all_left, sources)
        right_fresh = right_turn(right_hold, all_right, right_of)
        left_moved = from_behind(left_fresh, "site", 1)
        right_moved = from_behind(right_fresh, "site", -1)
        return (left_moved, right_moved, left_fresh)

    env_cur, env_right, env_next = lax.fori_loop(
        0, steps_total, chain_turn, (left_start, right_start, left_start)
    )
    trace_cur = trace_sum(env_cur)
    trace_next = trace_sum(env_next)
    trace_right = trace_sum(env_right)
    next_own = lax.dynamic_slice_in_dim(env_next, offset, owned, 0)
    right_own = lax.dynamic_slice_in_dim(env_right, offset, owned, 0)
    cur_scaled = (env_cur.astype(jnp.float32) * (dim_all / trace_cur)).astype(jnp.bfloat16)
    next_scaled = (next_own.astype(jnp.float32) * (dim_all / trace_next)).astype(jnp.bfloat16)
    right_scaled = (right_own.astype(jnp.float32) * (dim_all / trace_right)).astype(jnp.bfloat16)
    chosen_left = jnp.take(cur_scaled, own_sources, axis=0)
    for repeat in range(NAPP):
        half_site = jnp.einsum(
            "skab,skbc->skac", chosen_left, site_now, preferred_element_type=jnp.float32
        ).astype(jnp.bfloat16)
        site_now = (
            jnp.einsum(
                "skab,kbc->skac", half_site, right_scaled, preferred_element_type=jnp.float32
            )
            + energy[:, None, None, None] * site_now.astype(jnp.float32)
        ).astype(jnp.bfloat16)
        half_bond = jnp.einsum(
            "kab,kbc->kac", next_scaled, bond_now, preferred_element_type=jnp.float32
        ).astype(jnp.bfloat16)
        bond_now = (
            jnp.einsum("kab,kbc->kac", half_bond, right_scaled, preferred_element_type=jnp.float32)
            + bond_add * bond_now.astype(jnp.float32)
        ).astype(jnp.bfloat16)
    gram_left = jnp.einsum("skab,skac->kbc", site_now, site_now, preferred_element_type=jnp.float32)
    gram_bond = jnp.einsum("kab,kac->kbc", bond_now, bond_now, preferred_element_type=jnp.float32)
    unit_left = jnp.matmul(
        bond_now.astype(jnp.float32), inverse_root(gram_bond), precision=lax.Precision.HIGHEST
    )
    factor_left = jnp.matmul(
        inverse_root(gram_left), jnp.swapaxes(unit_left, -1, -2), precision=lax.Precision.HIGHEST
    ).astype(jnp.bfloat16)
    left_new = jnp.einsum(
        "skab,kbc->skac", site_now, factor_left, preferred_element_type=jnp.float32
    ).astype(jnp.bfloat16)
    outer_terms = jnp.einsum(
        "skab,skcb->skac", site_now, site_now, preferred_element_type=jnp.float32
    )
    routing = (own_sources[:, :, None] == labels[None, None, :]).astype(jnp.float32)
    buffer_all = jnp.einsum("skm,skac->mac", routing, outer_terms, precision=lax.Precision.HIGHEST)
    previous = from_behind(bond_now, "site", 1)
    gram_part = lax.psum_scatter(buffer_all, "sec", scatter_dimension=0, tiled=True)
    factor_part = right_polar(gram_part, previous)
    factor_right = lax.all_gather(factor_part, "sec", axis=0, tiled=True)
    factor_chosen = jnp.take(factor_right, own_sources, axis=0)
    right_new = jnp.einsum(
        "skab,skbc->skac", factor_chosen, site_now, preferred_element_type=jnp.float32
    ).astype(jnp.bfloat16)
    return (left_new[None], right_new[None])


def solution(mesh):
    return jax.shard_map(
        per_device,
        mesh=mesh,
        in_specs=(
            P("site", None, "sec", None, None),
            P("site", None, "sec", None, None),
            P("site", None, "sec", None, None),
            P("site", "sec", None, None),
            P("site", "sec", None, None),
            P("site", "sec", None, None),
            P("site", None, None),
            P("site", None),
            P("site"),
        ),
        out_specs=(P("site", None, "sec", None, None), P("site", None, "sec", None, None)),
        check_vma=False,
    )
```

profile of v0, /device:TPU:0, one launch (start us, length us, event | category | flops | bytes accessed | tf_op | source)
XLA Modules:
  0.0 190.5 jit_solution(11089584762305972886)
XLA Ops:
  8.0 10.2 %all-gather.3 = bf16[1,4,4,128,128]{4,3,2,1,0:T(8,128)(2,1)S(1)} all-gather(bf16[1,4,2,128,128]{4,3,2,1,0:T(8,128)(2,1)} %param.16), channel_id=5, replica_groups=mesh['site'=16,'sec'=2] {'sec'}, dimensions={2}, use_global_device_ids=true | all-gather | bytes 786432 | tf_op jit(solution)/shard_map/all_gather | solution.py:102
  18.3 5.1 %all-gather = bf16[1,4,128,128]{3,2,0,1:T(8,128)(2,1)S(1)} all-gather(bf16[1,2,128,128]{3,2,0,1:T(8,128)(2,1)} %bitcast.414), channel_id=2, replica_groups=mesh['site'=16,'sec'=2] {'sec'}, dimensions={1}, use_global_device_ids=true | all-gather | bytes 196608 | tf_op jit(solution)/shard_map/all_gather | solution.py:103
  24.3 7.2 %all-gather.2 = bf16[1,4,4,128,128]{4,3,2,1,0:T(8,128)(2,1)S(1)} all-gather(bf16[1,4,2,128,128]{4,3,2,1,0:T(8,128)(2,1)} %param.15), channel_id=4, replica_groups=mesh['site'=16,'sec'=2] {'sec'}, dimensions={2}, use_global_device_ids=true | all-gather | bytes 786432 | tf_op jit(solution)/shard_map/all_gather | solution.py:101
  31.5 5.1 %all-gather.1 = bf16[1,4,128,128]{3,2,0,1:T(8,128)(2,1)S(1)} all-gather(bf16[1,2,128,128]{3,2,0,1:T(8,128)(2,1)} %bitcast.415), channel_id=3, replica_groups=mesh['site'=16,'sec'=2] {'sec'}, dimensions={1}, use_global_device_ids=true | all-gather | bytes 196608 | tf_op jit(solution)/shard_map/all_gather | solution.py:104
  39.2 68.1 %while.16 = (s32[]{:T(128)}, bf16[4,128,128]{1,2,0:T(8,128)(2,1)S(1)}, bf16[4,128,128]{2,1,0:T(8,128)(2,1)S(1)}, bf16[4,128,128]{1,2,0:T(8,128)(2,1)}, s32[4,4]{...) while((s32[]{:T(128)}, ...), condition=%wide.region_2.0_spmd, body=%wide.region_1.3_spmd.sunk | while | flops 270016704 | bytes 9734929 | solution.py:115
  43.7 0.8 compare_and_fusion.15
  49.5 7.0 %collective-permute-done = bf16[4,128,128]{1,2,0:T(8,128)(2,1)S(1)} collective-permute-done((bf16[4,128,128]{1,2,0:T(8,128)(2,1)S(1)}, bf16[4,128,128]{1,2,0:T(8,128)(2,1)S(1)}, u32[]{:S(2)}, u32[]{:S(2)}) %collective-permute-start) | collective-permute-done | bytes 131104 | tf_op jit(solution)/shard_map/while/body/eval_jaxpr/ppermute | solution.py:13
  66.8 6.6 %collective-permute-done = bf16[4,128,128]{1,2,0:T(8,128)(2,1)S(1)} collective-permute-done((bf16[4,128,128]{1,2,0:T(8,128)(2,1)S(1)}, bf16[4,128,128]{1,2,0:T(8,128)(2,1)S(1)}, u32[]{:S(2)}, u32[]{:S(2)}) %collective-permute-start) | collective-permute-done | bytes 131104 | tf_op jit(solution)/shard_map/while/body/eval_jaxpr/ppermute | solution.py:13
  77.9 0.8 compare_and_fusion.15
  83.7 6.6 %collective-permute-done = bf16[4,128,128]{1,2,0:T(8,128)(2,1)S(1)} collective-permute-done((bf16[4,128,128]{1,2,0:T(8,128)(2,1)S(1)}, bf16[4,128,128]{1,2,0:T(8,128)(2,1)S(1)}, u32[]{:S(2)}, u32[]{:S(2)}) %collective-permute-start) | collective-permute-done | bytes 131104 | tf_op jit(solution)/shard_map/while/body/eval_jaxpr/ppermute | solution.py:13
  100.6 6.6 %collective-permute-done = bf16[4,128,128]{1,2,0:T(8,128)(2,1)S(1)} collective-permute-done((bf16[4,128,128]{1,2,0:T(8,128)(2,1)S(1)}, bf16[4,128,128]{1,2,0:T(8,128)(2,1)S(1)}, u32[]{:S(2)}, u32[]{:S(2)}) %collective-permute-start) | collective-permute-done | bytes 131104 | tf_op jit(solution)/shard_map/while/body/eval_jaxpr/ppermute | solution.py:13
  107.2 4.2 %copy.176 = f32[4,128,128]{0,2,1:T(8,128)} copy(bf16[4,128,128]{2,1,0:T(8,128)(2,1)S(1)} %get-tuple-element.113) | data formatting | bytes 393216 | tf_op jit(solution)/shard_map/convert_element_type | solution.py:31
  111.9 4.2 %copy.180 = f32[4,128,128]{0,2,1:T(8,128)} copy(bf16[4,128,128]{2,1,0:T(8,128)(2,1)S(1)} %copy.179) | data formatting | bytes 393216 | tf_op jit(solution)/shard_map/convert_element_type | solution.py:123
  116.0 1.8 gather_fusion.9
  119.4 1.8 gather_fusion.8
  124.6 0.9 convolution_bitcast_fusion.2
  126.3 7.3 %copy.189 = f32[4,128,128]{0,2,1:T(8,128)} copy(bf16[4,128,128]{1,2,0:T(8,128)(2,1)S(1)} %copy-done.1) | data formatting | bytes 393216 | tf_op jit(solution)/shard_map/convert_element_type | solution.py:31
  133.7 1.8 gather_fusion.10
  156.1 1.1 copy.203
  165.9 1.0 multiply_reduce_fusion
  166.9 1.3 fusion.100
  168.4 1.2 fusion.168
  177.1 4.9 %all_gather.19 = bf16[4,128,128]{2,1,0:T(8,128)(2,1)S(1)} all-gather(bf16[2,128,128]{2,1,0:T(8,128)(2,1)S(1)} %convolution_convert_fusion.12), channel_id=1, replica_groups=mesh['site'=16,'sec'=2] {'sec'}, dimensions={0}, use_global_device_ids=true | all-gather | bytes 196608 | tf_op jit(solution)/shard_map/all_gather | solution.py:163
  182.6 1.1 fusion.89
  (289 shorter events, 83.4 us)
Async XLA Ops:
  7.2 158.7 %reduce-scatter.2.cloned.1.call-start = ((), (), s32[]{:S(2)}) async-start(), calls=%async_computation.1 | async-start | bytes 393216 | tf_op jit(solution)/shard_map/reduce_scatter | solution.py:161
  43.6 5.9 %collective-permute-start.1 = (bf16[4,128,128]{2,1,0:T(8,128)(2,1)S(1)}, bf16[4,128,128]{2,1,0:T(8,128)(2,1)S(1)}, u32[]{:S(2)}, u32[]{:S(2)}) collective-permute-start(bf16[4,128,128]{2,1,0:T(8,128)(2,1)S(1)} %fusion.543), channel_id=1, source_target_pairs={{2,0},{4,2},{6,4},{8,6},{10,8},{12,10},{14,12},{16,14},{18,16},{20... | collective-permute-start | bytes 393224 | tf_op jit(solution)/shard_map/while/body/eval_jaxpr/ppermute | solution.py:13
  49.0 7.5 %copy-start = (bf16[4,128,128]{1,2,0:T(8,128)(2,1)}, bf16[4,128,128]{1,2,0:T(8,128)(2,1)S(1)}, u32[]{:S(2)}) copy-start(bf16[4,128,128]{1,2,0:T(8,128)(2,1)S(1)} %fusion.541) | copy-start | bytes 393220 | tf_op jit(solution)/shard_map/while
  49.0 7.5 %collective-permute-start = (bf16[4,128,128]{1,2,0:T(8,128)(2,1)S(1)}, bf16[4,128,128]{1,2,0:T(8,128)(2,1)S(1)}, u32[]{:S(2)}, u32[]{:S(2)}) collective-permute-start(bf16[4,128,128]{1,2,0:T(8,128)(2,1)S(1)} %fusion.541), channel_id=1, source_target_pairs={{30,0},{0,2},{2,4},{4,6},{6,8},{8,10},{10,12},{12,14},{14,16},{16,... | collective-permute-start | bytes 393224 | tf_op jit(solution)/shard_map/while/body/eval_jaxpr/ppermute | solution.py:13
  60.9 5.9 %collective-permute-start.1 = (bf16[4,128,128]{2,1,0:T(8,128)(2,1)S(1)}, bf16[4,128,128]{2,1,0:T(8,128)(2,1)S(1)}, u32[]{:S(2)}, u32[]{:S(2)}) collective-permute-start(bf16[4,128,128]{2,1,0:T(8,128)(2,1)S(1)} %fusion.543), channel_id=1, source_target_pairs={{2,0},{4,2},{6,4},{8,6},{10,8},{12,10},{14,12},{16,14},{18,16},{20... | collective-permute-start | bytes 393224 | tf_op jit(solution)/shard_map/while/body/eval_jaxpr/ppermute | solution.py:13
  66.2 7.2 %copy-start = (bf16[4,128,128]{1,2,0:T(8,128)(2,1)}, bf16[4,128,128]{1,2,0:T(8,128)(2,1)S(1)}, u32[]{:S(2)}) copy-start(bf16[4,128,128]{1,2,0:T(8,128)(2,1)S(1)} %fusion.541) | copy-start | bytes 393220 | tf_op jit(solution)/shard_map/while
  66.2 7.1 %collective-permute-start = (bf16[4,128,128]{1,2,0:T(8,128)(2,1)S(1)}, bf16[4,128,128]{1,2,0:T(8,128)(2,1)S(1)}, u32[]{:S(2)}, u32[]{:S(2)}) collective-permute-start(bf16[4,128,128]{1,2,0:T(8,128)(2,1)S(1)} %fusion.541), channel_id=1, source_target_pairs={{30,0},{0,2},{2,4},{4,6},{6,8},{8,10},{10,12},{12,14},{14,16},{16,... | collective-permute-start | bytes 393224 | tf_op jit(solution)/shard_map/while/body/eval_jaxpr/ppermute | solution.py:13
  77.8 5.9 %collective-permute-start.1 = (bf16[4,128,128]{2,1,0:T(8,128)(2,1)S(1)}, bf16[4,128,128]{2,1,0:T(8,128)(2,1)S(1)}, u32[]{:S(2)}, u32[]{:S(2)}) collective-permute-start(bf16[4,128,128]{2,1,0:T(8,128)(2,1)S(1)} %fusion.543), channel_id=1, source_target_pairs={{2,0},{4,2},{6,4},{8,6},{10,8},{12,10},{14,12},{16,14},{18,16},{20... | collective-permute-start | bytes 393224 | tf_op jit(solution)/shard_map/while/body/eval_jaxpr/ppermute | solution.py:13
  83.2 7.2 %copy-start = (bf16[4,128,128]{1,2,0:T(8,128)(2,1)}, bf16[4,128,128]{1,2,0:T(8,128)(2,1)S(1)}, u32[]{:S(2)}) copy-start(bf16[4,128,128]{1,2,0:T(8,128)(2,1)S(1)} %fusion.541) | copy-start | bytes 393220 | tf_op jit(solution)/shard_map/while
  83.2 7.1 %collective-permute-start = (bf16[4,128,128]{1,2,0:T(8,128)(2,1)S(1)}, bf16[4,128,128]{1,2,0:T(8,128)(2,1)S(1)}, u32[]{:S(2)}, u32[]{:S(2)}) collective-permute-start(bf16[4,128,128]{1,2,0:T(8,128)(2,1)S(1)} %fusion.541), channel_id=1, source_target_pairs={{30,0},{0,2},{2,4},{4,6},{6,8},{8,10},{10,12},{12,14},{14,16},{16,... | collective-permute-start | bytes 393224 | tf_op jit(solution)/shard_map/while/body/eval_jaxpr/ppermute | solution.py:13
  94.8 5.9 %collective-permute-start.1 = (bf16[4,128,128]{2,1,0:T(8,128)(2,1)S(1)}, bf16[4,128,128]{2,1,0:T(8,128)(2,1)S(1)}, u32[]{:S(2)}, u32[]{:S(2)}) collective-permute-start(bf16[4,128,128]{2,1,0:T(8,128)(2,1)S(1)} %fusion.543), channel_id=1, source_target_pairs={{2,0},{4,2},{6,4},{8,6},{10,8},{12,10},{14,12},{16,14},{18,16},{20... | collective-permute-start | bytes 393224 | tf_op jit(solution)/shard_map/while/body/eval_jaxpr/ppermute | solution.py:13
  100.1 7.2 %copy-start = (bf16[4,128,128]{1,2,0:T(8,128)(2,1)}, bf16[4,128,128]{1,2,0:T(8,128)(2,1)S(1)}, u32[]{:S(2)}) copy-start(bf16[4,128,128]{1,2,0:T(8,128)(2,1)S(1)} %fusion.541) | copy-start | bytes 393220 | tf_op jit(solution)/shard_map/while
  100.1 7.1 %collective-permute-start = (bf16[4,128,128]{1,2,0:T(8,128)(2,1)S(1)}, bf16[4,128,128]{1,2,0:T(8,128)(2,1)S(1)}, u32[]{:S(2)}, u32[]{:S(2)}) collective-permute-start(bf16[4,128,128]{1,2,0:T(8,128)(2,1)S(1)} %fusion.541), channel_id=1, source_target_pairs={{30,0},{0,2},{2,4},{4,6},{6,8},{8,10},{10,12},{12,14},{14,16},{16,... | collective-permute-start | bytes 393224 | tf_op jit(solution)/shard_map/while/body/eval_jaxpr/ppermute | solution.py:13
  107.2 4.3 %copy-start.3 = (s32[4,4]{1,0:T(4,128)S(1)}, s32[4,4]{1,0:T(4,128)}, u32[]{:S(2)}) copy-start(s32[4,4]{1,0:T(4,128)} %get-tuple-element.412) | copy-start | bytes 196
  107.2 15.3 %copy-start.2 = (bf16[1,4,2,128,128]{4,3,2,1,0:T(8,128)(2,1)S(1)}, bf16[1,4,2,128,128]{4,3,2,1,0:T(8,128)(2,1)}, u32[]{:S(2)}) copy-start(bf16[1,4,2,128,128]{4,3,2,1,0:T(8,128)(2,1)} %param.17) | copy-start | bytes 786436
  107.2 16.1 %copy-start.5 = (f32[1,4]{1,0:T(1,128)S(1)}, f32[1,4]{1,0:T(1,128)}, u32[]{:S(2)}) copy-start(f32[1,4]{1,0:T(1,128)} %param.22) | copy-start | bytes 52
  111.4 14.8 %copy-start.1 = (bf16[4,128,128]{1,2,0:T(8,128)(2,1)S(1)}, bf16[4,128,128]{1,2,0:T(8,128)(2,1)}, u32[]{:S(2)}) copy-start(bf16[4,128,128]{1,2,0:T(8,128)(2,1)} %get-tuple-element.115) | copy-start | bytes 393220
  116.0 21.4 %copy-start.4 = (bf16[1,2,128,128]{3,2,1,0:T(8,128)(2,1)S(1)}, bf16[1,2,128,128]{3,2,1,0:T(8,128)(2,1)}, u32[]{:S(2)}) copy-start(bf16[1,2,128,128]{3,2,1,0:T(8,128)(2,1)} %param.18) | copy-start | bytes 196612
  138.0 19.1 %collective-permute-start.2 = (bf16[2,128,128]{2,1,0:T(8,128)(2,1)S(1)}, bf16[2,128,128]{2,1,0:T(8,128)(2,1)S(1)}, u32[]{:S(2)}, u32[]{:S(2)}) collective-permute-start(bf16[2,128,128]{2,1,0:T(8,128)(2,1)S(1)} %fusion.132), channel_id=1, source_target_pairs={{30,0},{0,2},{2,4},{4,6},{6,8},{8,10},{10,12},{12,14},{14,16},{16,... | collective-permute-start | bytes 196616 | tf_op jit(solution)/shard_map/ppermute | solution.py:13
Sparse Core Ops, SparseCore 0:
  126.4 9.0 reduce-scatter.1
where the time goes:
time: 191 us
  matrix products  55.8 us (29%)
  local copies, waits for them, and re-layouts  46.5 us (24%)
  blocking collectives  32.7 us (17%)
  waiting for transfers between devices  26.8 us (14%)
  between operations  18 us (9%)
  other arithmetic  7.46 us (4%)
  starting transfers between devices  2.68 us (1%)
    ppermute x9, waiting for transfers between devices, from_behind(): return lax.ppermute(block, axis, route)  26.7 us
    dot_general x40, matrix products, inverse_root(): jnp.matmul(lower_part, upper_part, precision=lax.Precision.HIGHEST)  12 us
    convert_element_type x2, local copies, waits for them, and re-layouts, trace_sum(): return jnp.sum(jnp.diagonal(blocks.astype(jnp.float32), axis1=1, axis2=2))  11.5 us
    dot_general x36, matrix products, inverse_root(): upper_part = jnp.matmul(upper_part, middle, precision=lax.Precision.HIGHEST)  10.7 us
    dot_general x40, matrix products, inverse_root(): lower_part = jnp.matmul(middle, lower_part, precision=lax.Precision.HIGHEST)  10.7 us
    all_gather x1, blocking collectives, per_device(): lax.all_gather(canon_right, 'sec', axis=1, tiled=True)  10.2 us
    gather x16, local copies, waits for them, and re-layouts, left_turn(): chosen = jnp.take(hold_full, indices[physical], axis=0)  9.15 us
    gather x16, local copies, waits for them, and re-layouts, right_turn(): env_chosen = jnp.take(hold_full, indices[physical], axis=0)  9.15 us
  transfers between devices with their start and end apart: 10, of which 4 were waited for; matrix products, arithmetic and copies ran while one was open for 30% of the time, Pallas kernels for 0%

commit v1 on v0

v1 whole, which is shorter than its diff:
```python
import functools

import jax
import jax.numpy as jnp
from jax import lax
from jax.experimental import pallas as pl
from jax.experimental.pallas import tpu as pltpu
from jax.sharding import PartitionSpec as P

NSI = 10
NAPP = 2
MESH = pl.DeviceIdType.MESH
F32 = jnp.float32
BF16 = jnp.bfloat16


def dot(a, b):
    return lax.dot_general(a, b, (((1,), (0,)), ((), ())), preferred_element_type=F32)


def dot_nt(a, b):
    return lax.dot_general(a, b, (((1,), (1,)), ((), ())), preferred_element_type=F32)


def dot_tn(a, b):
    return lax.dot_general(a, b, (((0,), (0,)), ((), ())), preferred_element_type=F32)


def split(x):
    hi = x.astype(BF16)
    return hi, (x - hi.astype(F32)).astype(BF16)


def as_lhs(pair):
    return jnp.concatenate(pair, axis=1)


def as_rhs(pair):
    row = jnp.concatenate(pair, axis=1)
    return jnp.concatenate((row, row), axis=0)


def mm(lhs_pair, rhs_pair):
    out = dot(as_lhs(lhs_pair), as_rhs(rhs_pair))
    width = out.shape[1] // 2
    return out[:, :width] + out[:, width:]


def kernel(
    steps, sites, parts, phys, owned,
    lc, rc, cs, cb, lseed, rseed, src, onsite, shift,
    left_new, right_new,
    hold_l, lrecv, lsend, rrecv, psend, terms, lct, site, bond, ys, zs, env_r, env_n,
    gsend, grecv, usend, urecv, fsend, frecv, fall, tns, tnr, trs, trr,
    s_ls, s_lr, s_ps, s_pr, s_gs, s_gr, s_us, s_ur, s_fs, s_fr, s_tns, s_tnr, s_trs, s_trr,
):
    j = lax.axis_index("site")
    me = lax.axis_index("sec")
    after, before = lax.rem(j + 1, sites), lax.rem(j + sites - 1, sites)
    off = me * owned
    width = lc.shape[-1]
    sectors = parts * owned

    def sec(d):
        return lax.rem(me + d, parts)

    def copy(a, b, ss, rs, to_site, to_sec):
        return pltpu.make_async_remote_copy(
            src_ref=a, dst_ref=b, send_sem=ss, recv_sem=rs,
            device_id={"site": to_site, "sec": to_sec}, device_id_type=MESH,
        )

    def c_seed(d):
        return copy(lseed.at[0], lrecv.at[0, me], s_ls.at[steps, d], s_lr.at[0, me], j, sec(d))

    def c_left(t, d):
        return copy(lsend.at[t], lrecv.at[t + 1, me], s_ls.at[t, d], s_lr.at[t + 1, me], after, sec(d))

    def c_right(t, d):
        return copy(psend.at[t, d], rrecv.at[t, me], s_ps.at[t, d], s_pr.at[t, me], before, sec(d))

    def c_tn(d):
        return copy(tns, tnr.at[me], s_tns.at[d], s_tnr.at[me], j, sec(d))

    def c_tr(d):
        return copy(trs, trr.at[me], s_trs.at[d], s_trr.at[me], before, sec(d))

    def c_gram(d):
        return copy(gsend.at[d], grecv.at[me], s_gs.at[d], s_gr.at[me], j, sec(d))

    def c_unit():
        return copy(usend, urecv, s_us.at[0], s_ur.at[0], after, me)

    def c_factor(d):
        return copy(fsend, frecv.at[me], s_fs.at[d], s_fr.at[me], j, sec(d))

    def got(ref, sem):
        copy(ref, ref, s_us.at[0], sem, after, me).wait_recv()

    barrier = pltpu.get_barrier_semaphore()
    for d in range(parts):
        for where in (after, before) if d == 0 else (after, before, j):
            pl.semaphore_signal(
                barrier, inc=1, device_id={"site": where, "sec": sec(d)}, device_id_type=MESH
            )
    pl.semaphore_wait(barrier, 3 * parts - 1)

    for d in range(1, parts):
        c_seed(d).start()

    sources = [[src[0, s, off + k] for k in range(owned)] for s in range(phys)]

    def gathered(target, i):
        want = target * owned + i
        total = None
        for s in range(phys):
            hit, at = jnp.int32(0), jnp.int32(0)
            for k in range(owned):
                same = (sources[s][k] == want).astype(jnp.int32)
                hit, at = hit + same, at + same * k
            term = terms[s * owned + at] * hit.astype(F32)
            total = term if total is None else total + term
        return total

    for k in range(owned):
        for s in range(phys):
            lct[k, :, s * width : (s + 1) * width] = lc[0, s, k].T
    for k in range(owned):
        env_r[k] = rseed[0, k]
        hold_l[off + k] = lseed[0, k]
    for d in range(1, parts):
        a = sec(d)
        got(lrecv.at[0, a], s_lr.at[0, a])
        for k in range(owned):
            hold_l[a * owned + k] = lrecv[0, a, k]

    def left_arrival(t):
        for d in range(parts):
            a = sec(d)
            got(lrecv.at[t, a], s_lr.at[t, a])
            for k in range(owned):
                hold_l[a * owned + k] = lrecv[t, a, k]

    def right_arrival(t):
        for d in range(parts):
            a = sec(d)
            got(rrecv.at[t, a], s_pr.at[t, a])
        for k in range(owned):
            total = rrecv[t, 0, k].astype(F32)
            for a in range(1, parts):
                total = total + rrecv[t, a, k].astype(F32)
            env_r[k] = total.astype(BF16)

    def turn(t, carry):
        for k in range(owned):
            prods = [
                dot(hold_l[sources[s][k]], lc[0, s, k]).astype(BF16) for s in range(phys)
            ]
            lsend[t, k] = dot(lct[k], jnp.concatenate(prods, axis=0)).astype(BF16)
        for d in range(parts):
            c_left(t, d).start()

        @pl.when(t > 0)
        def _():
            right_arrival(t - 1)

        for k in range(owned):
            stack = jnp.concatenate([rc[0, s, k] for s in range(phys)], axis=0)
            prod = dot(stack, env_r[k]).astype(BF16)
            for s in range(phys):
                terms[s * owned + k] = dot_nt(prod[s * width : (s + 1) * width], rc[0, s, k])
        for d in range(parts):
            for i in range(owned):
                psend[t, d, i] = gathered(sec(d), i).astype(BF16)
            c_right(t, d).start()

        @pl.when(t < steps - 1)
        def _():
            left_arrival(t + 1)

        return carry

    lax.fori_loop(0, steps, turn, 0)

    rows = lax.broadcasted_iota(jnp.int32, (width, width), 0)
    cols = lax.broadcasted_iota(jnp.int32, (width, width), 1)
    diagonal = (rows == cols).astype(F32)

    def traces(blocks):
        total = None
        for block in blocks:
            total = block.astype(F32) if total is None else total + block.astype(F32)
        return jnp.sum((total * diagonal).reshape(width // 8, 8, width), axis=0)

    tns[...] = traces([lsend[steps - 1, k] for k in range(owned)])
    for d in range(1, parts):
        c_tn(d).start()
    trs[...] = traces([psend[steps - 1, d, i] for d in range(parts) for i in range(owned)])
    for d in range(parts):
        c_tr(d).start()

    def scale_of(total):
        return (sectors * width) / jnp.sum(total, axis=(0, 1), keepdims=True)

    total = tns[...]
    for d in range(1, parts):
        a = sec(d)
        got(tnr.at[a], s_tnr.at[a])
        total = total + tnr[a]
    scale = scale_of(total)
    for k in range(owned):
        env_n[k] = (lsend[steps - 1, k].astype(F32) * scale).astype(BF16)

    left_arrival(steps)
    scale = scale_of(traces([hold_l[m] for m in range(sectors)]))
    for m in range(sectors):
        hold_l[m] = (hold_l[m].astype(F32) * scale).astype(BF16)

    right_arrival(steps - 1)
    for a in range(parts):
        got(trr.at[a], s_trr.at[a])
    total = trr[0]
    for a in range(1, parts):
        total = total + trr[a]
    scale = scale_of(total)
    for k in range(owned):
        env_r[k] = (env_r[k].astype(F32) * scale).astype(BF16)

    for k in range(owned):
        for s in range(phys):
            site[k, s * width : (s + 1) * width] = cs[0, s, k]
        bond[k] = cb[0, k]
    for repeat in range(NAPP):
        for k in range(owned):
            halves = [
                dot(hold_l[sources[s][k]], site[k, s * width : (s + 1) * width]).astype(BF16)
                for s in range(phys)
            ]
            whole = dot(jnp.concatenate(halves, axis=0), env_r[k])
            for s in range(phys):
                part = slice(s * width, (s + 1) * width)
                site[k, part] = (whole[part] + onsite[0, s] * site[k, part].astype(F32)).astype(BF16)

    for k in range(owned):
        for s in range(phys):
            block = site[k, s * width : (s + 1) * width]
            terms[s * owned + k] = dot_nt(block, block)
    for d in range(parts - 1, -1, -1):
        for i in range(owned):
            gsend[d, i] = gathered(sec(d), i)
        if d > 0:
            c_gram(d).start()

    for repeat in range(NAPP):
        for k in range(owned):
            half = dot(env_n[k], bond[k]).astype(BF16)
            bond[k] = (dot(half, env_r[k]) + shift[0] * bond[k].astype(F32)).astype(BF16)

    def inverse_roots(grams):
        norms = []
        for i, gram in enumerate(grams):
            norm = jnp.sqrt(jnp.sum(gram * gram, axis=(0, 1), keepdims=True))
            norms.append(norm)
            upper = gram / norm
            middle = 1.5 * diagonal - 0.5 * upper
            ys[i] = mm(split(upper), split(middle))
            zs[i] = middle

        def body(n, carry):
            uppers = [split(ys[i]) for i in range(len(grams))]
            lowers = [split(zs[i]) for i in range(len(grams))]
            middles = [
                split(1.5 * diagonal - 0.5 * mm(z, y)) for z, y in zip(lowers, uppers)
            ]
            for i in range(len(grams)):
                ys[i] = mm(uppers[i], middles[i])
                zs[i] = mm(middles[i], lowers[i])
            return carry

        lax.fori_loop(0, NSI - 2, body, 0)
        for i in range(len(grams)):
            lower = split(zs[i])
            middle = split(1.5 * diagonal - 0.5 * mm(lower, split(ys[i])))
            zs[i] = mm(middle, lower) / jnp.sqrt(norms[i])

    inverse_roots(
        [dot_tn(bond[k], bond[k]) for k in range(owned)]
        + [dot_tn(site[k], site[k]) for k in range(owned)]
    )
    factors = []
    for k in range(owned):
        hi, lo = split(zs[k])
        unit_t = dot_nt(hi, bond[k]) + dot_nt(lo, bond[k])
        usend[k] = unit_t.astype(BF16)
        factors.append(mm(split(zs[owned + k]), split(unit_t)).astype(BF16))
    c_unit().start()

    for d in range(1, parts):
        a = sec(d)
        got(grecv.at[a], s_gr.at[a])
    grams = []
    for i in range(owned):
        total = gsend[0, i]
        for d in range(1, parts):
            total = total + grecv[sec(d), i]
        grams.append(total)
    inverse_roots(grams)
    got(urecv, s_ur.at[0])
    for i in range(owned):
        hi, lo = split(zs[i])
        fsend[i] = (dot(urecv[i], hi) + dot(urecv[i], lo)).astype(BF16)
    for d in range(1, parts):
        c_factor(d).start()

    for k in range(owned):
        whole = dot(site[k], factors[k]).astype(BF16)
        for s in range(phys):
            left_new[0, s, k] = whole[s * width : (s + 1) * width]
    for i in range(owned):
        fall[off + i] = fsend[i]
    for d in range(1, parts):
        a = sec(d)
        got(frecv.at[a], s_fr.at[a])
        for i in range(owned):
            fall[a * owned + i] = frecv[a, i]
    for k in range(owned):
        for s in range(phys):
            block = site[k, s * width : (s + 1) * width]
            right_new[0, s, k] = dot(fall[sources[s][k]], block).astype(BF16)

    def drain(t, carry):
        for d in range(parts):
            c_left(t, d).wait_send()
            c_right(t, d).wait_send()
        return carry

    lax.fori_loop(0, steps, drain, 0)
    for d in range(parts):
        c_tr(d).wait_send()
    for d in range(1, parts):
        for c in (c_seed, c_tn, c_gram, c_factor):
            c(d).wait_send()
    c_unit().wait_send()


def per_device(lc, rc, cs, cb, lseed, rseed, src, onsite, shift):
    sites, parts = lax.axis_size("site"), lax.axis_size("sec")
    steps = sites // 4
    _, phys, owned, width, _ = lc.shape
    sectors = parts * owned
    block = (width, width)
    most = 2 * owned

    def vm(*shape, dtype=BF16):
        return pltpu.VMEM(shape, dtype)

    def dma(*shape):
        return pltpu.SemaphoreType.DMA(shape)

    in_vmem = pl.BlockSpec(memory_space=pltpu.VMEM)
    in_smem = pl.BlockSpec(memory_space=pltpu.SMEM)
    shape = jax.ShapeDtypeStruct(cs.shape, BF16)
    return pl.pallas_call(
        functools.partial(kernel, steps, sites, parts, phys, owned),
        out_shape=(shape, shape),
        in_specs=[in_vmem] * 6 + [in_smem] * 3,
        out_specs=(in_vmem, in_vmem),
        scratch_shapes=[
            vm(sectors, *block),
            vm(steps + 1, parts, owned, *block),
            vm(steps, owned, *block),
            vm(steps, parts, owned, *block),
            vm(steps, parts, owned, *block),
            vm(phys * owned, *block, dtype=F32),
            vm(owned, width, phys * width),
            vm(owned, phys * width, width),
            vm(owned, *block),
            vm(most, *block, dtype=F32),
            vm(most, *block, dtype=F32),
            vm(owned, *block),
            vm(owned, *block),
            vm(parts, owned, *block, dtype=F32),
            vm(parts, owned, *block, dtype=F32),
            vm(owned, *block),
            vm(owned, *block),
            vm(owned, *block),
            vm(parts, owned, *block),
            vm(sectors, *block),
            vm(8, width, dtype=F32),
            vm(parts, 8, width, dtype=F32),
            vm(8, width, dtype=F32),
            vm(parts, 8, width, dtype=F32),
            dma(steps + 1, parts), dma(steps + 1, parts),
            dma(steps, parts), dma(steps, parts),
            dma(parts), dma(parts),
            dma(1), dma(1),
            dma(parts), dma(parts),
            dma(parts), dma(parts),
            dma(parts), dma(parts),
        ],
        compiler_params=pltpu.CompilerParams(
            collective_id=0, has_side_effects=True, vmem_limit_bytes=60 * 1024 * 1024
        ),
    )(lc, rc, cs, cb, lseed, rseed, src, onsite, shift)


def solution(mesh):
    tensor = P("site", None, "sec", None, None)
    blocks = P("site", "sec", None, None)
    return jax.shard_map(
        per_device,
        mesh=mesh,
        in_specs=(tensor, tensor, tensor, blocks, blocks, blocks,
                  P("site", None, None), P("site", None), P("site")),
        out_specs=(tensor, tensor),
        check_vma=False,
    )
```

time: 191 us -> 50.9 us (0.27)
  matrix products: 55.8 us -> 0 us
  Pallas kernels: 0 us -> 47 us
  local copies, waits for them, and re-layouts: 46.5 us -> 2.42 us
  blocking collectives: 32.7 us -> 0 us
  waiting for transfers between devices: 26.8 us -> 0 us
  between operations: 18 us -> 1.3 us
  other arithmetic: 7.46 us -> 0 us
  starting transfers between devices: 2.68 us -> 0 us
    dot_general x163 -> x0, matrix products: 55.8 us -> none  [the longest x40 12 us: inverse_root(): jnp.matmul(lower_part, upper_part, precision=lax.Precision.HIGHEST)]
    pallas_call x0 -> x1, Pallas kernels: none -> 47 us  [per_device(): pl.pallas_call(functools.partial(kernel, steps, sites, parts, phys, owned...]
    all_gather x5 -> x0, blocking collectives: 32.7 us -> none  [the longest x1 10.2 us: per_device(): lax.all_gather(canon_right, 'sec', axis=1, tiled=True)]
    gather x41 -> x0, local copies, waits for them, and re-layouts: 27.1 us -> none  [the longest x16 9.15 us: left_turn(): chosen = jnp.take(hold_full, indices[physical], axis=0)]
    ppermute x9 -> x0, waiting for transfers between devices: 26.7 us -> none  [from_behind(): return lax.ppermute(block, axis, route)]
    convert_element_type x3 -> x0, local copies, waits for them, and re-layouts: 15.6 us -> none  [the longest x2 11.5 us: trace_sum(): return jnp.sum(jnp.diagonal(blocks.astype(jnp.float32), axis1=1, axis2=2))]
    reduce_sum x5 -> x0, other arithmetic: 3.64 us -> none  [the longest x3 1.85 us: trace_sum(): return jnp.sum(jnp.diagonal(blocks.astype(jnp.float32), axis1=1, axis2=2))]
    and x10 -> x0, other arithmetic: 3.43 us -> none  [the longest x4 3.37 us: left_turn(): chosen = jnp.take(hold_full, indices[physical], axis=0)]
  transfers between devices with their start and end apart: 10 -> 0, of which waited for: 4 -> 0; matrix products, arithmetic and copies ran while one was open for 30% -> 0% of each run, Pallas kernels for 0% -> 0%
where the time goes in v1:
time: 50.9 us; the launch traced here: 50.7 us
  Pallas kernels  47 us (92%)
  local copies, waits for them, and re-layouts  2.42 us (5%)
  between operations  1.3 us (3%)
    pallas_call x1, Pallas kernels, per_device(): pl.pallas_call(functools.partial(kernel, steps, sites, parts, phys, owned...  47 us
    unnamed x4, local copies, waits for them, and re-layouts  2.42 us

profile of v1, /device:TPU:0, one launch (start us, length us, event | category | flops | bytes accessed | tf_op | source)
XLA Modules:
  0.0 50.7 jit_solution(11100125022548570329)
XLA Ops:
  1.3 47.0 %shard_map.104 = (bf16[1,4,2,128,128]{4,3,2,1,0:T(8,128)(2,1)}, bf16[1,4,2,128,128]{4,3,2,1,0:T(8,128)(2,1)}) custom-call(bf16[1,4,2,128,128]{4,3,2,1,0:T(8,128)(2,1)} %lc.1, bf16[1,4,2,128,128]{4,3,2,1,0:T(8,128)(2,1)} %rc.1, bf16[1,4,2,128,128]{4,3,2,1,0:T(8,128)(2,1)} %cs.1, bf16[1,2,128,128]{3,2,1,0:T(8,128)(2,1)} %cb.1, bf16[1,2,128,128]{3,2,1,0:T(8,128)(2,1)} %lseed.1, ...), custom_call_target="tpu_custom_call" | custom-call | tf_op jit(solution)/shard_map/pallas_call | solution.py:363
  48.3 0.0 copy-start
  48.3 1.7 %copy.14 = bf16[1,4,2,128,128]{4,3,2,1,0:T(8,128)(2,1)} copy(bf16[1,4,2,128,128]{4,3,2,1,0:T(8,128)(2,1)} %get-tuple-element.4) | data formatting | bytes 524288
  50.0 0.0 copy-done
  50.0 0.7 %copy.15 = bf16[1,4,2,128,128]{4,3,2,1,0:T(8,128)(2,1)} copy(bf16[1,4,2,128,128]{4,3,2,1,0:T(8,128)(2,1)S(1)} %copy-done) | data formatting | bytes 524288
Async XLA Ops:
  48.3 1.7 %copy-start = (bf16[1,4,2,128,128]{4,3,2,1,0:T(8,128)(2,1)S(1)}, bf16[1,4,2,128,128]{4,3,2,1,0:T(8,128)(2,1)}, u32[]{:S(2)}) copy-start(bf16[1,4,2,128,128]{4,3,2,1,0:T(8,128)(2,1)} %get-tuple-element.5) | copy-start | bytes 786436

commit v2 on v1

--- a/solution.py
+++ b/solution.py
@@ -128,11 +128,12 @@
     for k in range(owned):
         env_r[k] = rseed[0, k]
         hold_l[off + k] = lseed[0, k]
-    for d in range(1, parts):
-        a = sec(d)
-        got(lrecv.at[0, a], s_lr.at[0, a])
-        for k in range(owned):
-            hold_l[a * owned + k] = lrecv[0, a, k]
+    def seed_arrival():
+        for d in range(1, parts):
+            a = sec(d)
+            got(lrecv.at[0, a], s_lr.at[0, a])
+            for k in range(owned):
+                hold_l[a * owned + k] = lrecv[0, a, k]
 
     def left_arrival(t):
         for d in range(parts):
@@ -152,14 +153,6 @@
             env_r[k] = total.astype(BF16)
 
     def turn(t, carry):
-        for k in range(owned):
-            prods = [
-                dot(hold_l[sources[s][k]], lc[0, s, k]).astype(BF16) for s in range(phys)
-            ]
-            lsend[t, k] = dot(lct[k], jnp.concatenate(prods, axis=0)).astype(BF16)
-        for d in range(parts):
-            c_left(t, d).start()
-
         @pl.when(t > 0)
         def _():
             right_arrival(t - 1)
@@ -174,9 +167,21 @@
                 psend[t, d, i] = gathered(sec(d), i).astype(BF16)
             c_right(t, d).start()
 
-        @pl.when(t < steps - 1)
+        @pl.when(t == 0)
         def _():
-            left_arrival(t + 1)
+            seed_arrival()
+
+        @pl.when(t > 0)
+        def _():
+            left_arrival(t)
+
+        for k in range(owned):
+            prods = [
+                dot(hold_l[sources[s][k]], lc[0, s, k]).astype(BF16) for s in range(phys)
+            ]
+            lsend[t, k] = dot(lct[k], jnp.concatenate(prods, axis=0)).astype(BF16)
+        for d in range(parts):
+            c_left(t, d).start()
 
         return carry
 

time: 50.9 us -> 49.7 us (0.976)
  Pallas kernels: 47 us -> 45.8 us
    pallas_call x1, Pallas kernels: 47 us -> 45.8 us  [per_device(): pl.pallas_call(functools.partial(kernel, steps, sites, parts, phys, owned...]
where the time goes in v2:
time: 49.7 us; the launch traced here: 49.5 us
  Pallas kernels  45.8 us (92%)
  local copies, waits for them, and re-layouts  2.42 us (5%)
  between operations  1.3 us (3%)
    pallas_call x1, Pallas kernels, per_device(): pl.pallas_call(functools.partial(kernel, steps, sites, parts, phys, owned...  45.8 us
    unnamed x4, local copies, waits for them, and re-layouts  2.42 us

profile of v2, /device:TPU:0, one launch (start us, length us, event | category | flops | bytes accessed | tf_op | source)
XLA Modules:
  0.0 49.5 jit_solution(5098223935879853678)
XLA Ops:
  1.3 45.8 %shard_map.104 = (bf16[1,4,2,128,128]{4,3,2,1,0:T(8,128)(2,1)}, bf16[1,4,2,128,128]{4,3,2,1,0:T(8,128)(2,1)}) custom-call(bf16[1,4,2,128,128]{4,3,2,1,0:T(8,128)(2,1)} %lc.1, bf16[1,4,2,128,128]{4,3,2,1,0:T(8,128)(2,1)} %rc.1, bf16[1,4,2,128,128]{4,3,2,1,0:T(8,128)(2,1)} %cs.1, bf16[1,2,128,128]{3,2,1,0:T(8,128)(2,1)} %cb.1, bf16[1,2,128,128]{3,2,1,0:T(8,128)(2,1)} %lseed.1, ...), custom_call_target="tpu_custom_call" | custom-call | tf_op jit(solution)/shard_map/pallas_call | solution.py:368
  47.1 0.0 copy-start
  47.1 1.7 %copy.14 = bf16[1,4,2,128,128]{4,3,2,1,0:T(8,128)(2,1)} copy(bf16[1,4,2,128,128]{4,3,2,1,0:T(8,128)(2,1)} %get-tuple-element.4) | data formatting | bytes 524288
  48.8 0.0 copy-done
  48.8 0.7 %copy.15 = bf16[1,4,2,128,128]{4,3,2,1,0:T(8,128)(2,1)} copy(bf16[1,4,2,128,128]{4,3,2,1,0:T(8,128)(2,1)S(1)} %copy-done) | data formatting | bytes 524288
Async XLA Ops:
  47.1 1.7 %copy-start = (bf16[1,4,2,128,128]{4,3,2,1,0:T(8,128)(2,1)S(1)}, bf16[1,4,2,128,128]{4,3,2,1,0:T(8,128)(2,1)}, u32[]{:S(2)}) copy-start(bf16[1,4,2,128,128]{4,3,2,1,0:T(8,128)(2,1)} %get-tuple-element.5) | copy-start | bytes 786436

commit v3 on v2

--- a/solution.py
+++ b/solution.py
@@ -162,7 +162,7 @@
             prod = dot(stack, env_r[k]).astype(BF16)
             for s in range(phys):
                 terms[s * owned + k] = dot_nt(prod[s * width : (s + 1) * width], rc[0, s, k])
-        for d in range(parts):
+        for d in reversed(range(parts)):
             for i in range(owned):
                 psend[t, d, i] = gathered(sec(d), i).astype(BF16)
             c_right(t, d).start()
@@ -180,7 +180,7 @@
                 dot(hold_l[sources[s][k]], lc[0, s, k]).astype(BF16) for s in range(phys)
             ]
             lsend[t, k] = dot(lct[k], jnp.concatenate(prods, axis=0)).astype(BF16)
-        for d in range(parts):
+        for d in reversed(range(parts)):
             c_left(t, d).start()
 
         return carry

time: 49.7 us -> 49.7 us (level)
  no operation moved by 1% of the time
where the time goes in v3:
time: 49.7 us; the launch traced here: 49.6 us
  Pallas kernels  45.9 us (92%)
  local copies, waits for them, and re-layouts  2.42 us (5%)
  between operations  1.3 us (3%)
    pallas_call x1, Pallas kernels, per_device(): pl.pallas_call(functools.partial(kernel, steps, sites, parts, phys, owned...  45.9 us
    unnamed x4, local copies, waits for them, and re-layouts  2.42 us

profile of v3, /device:TPU:0, one launch (start us, length us, event | category | flops | bytes accessed | tf_op | source)
XLA Modules:
  0.0 49.6 jit_solution(18249929879044031384)
XLA Ops:
  1.3 45.9 %shard_map.104 = (bf16[1,4,2,128,128]{4,3,2,1,0:T(8,128)(2,1)}, bf16[1,4,2,128,128]{4,3,2,1,0:T(8,128)(2,1)}) custom-call(bf16[1,4,2,128,128]{4,3,2,1,0:T(8,128)(2,1)} %lc.1, bf16[1,4,2,128,128]{4,3,2,1,0:T(8,128)(2,1)} %rc.1, bf16[1,4,2,128,128]{4,3,2,1,0:T(8,128)(2,1)} %cs.1, bf16[1,2,128,128]{3,2,1,0:T(8,128)(2,1)} %cb.1, bf16[1,2,128,128]{3,2,1,0:T(8,128)(2,1)} %lseed.1, ...), custom_call_target="tpu_custom_call" | custom-call | tf_op jit(solution)/shard_map/pallas_call | solution.py:368
  47.2 0.0 copy-start
  47.2 1.7 %copy.14 = bf16[1,4,2,128,128]{4,3,2,1,0:T(8,128)(2,1)} copy(bf16[1,4,2,128,128]{4,3,2,1,0:T(8,128)(2,1)} %get-tuple-element.4) | data formatting | bytes 524288
  48.9 0.0 copy-done
  48.9 0.7 %copy.15 = bf16[1,4,2,128,128]{4,3,2,1,0:T(8,128)(2,1)} copy(bf16[1,4,2,128,128]{4,3,2,1,0:T(8,128)(2,1)S(1)} %copy-done) | data formatting | bytes 524288
Async XLA Ops:
  47.2 1.7 %copy-start = (bf16[1,4,2,128,128]{4,3,2,1,0:T(8,128)(2,1)S(1)}, bf16[1,4,2,128,128]{4,3,2,1,0:T(8,128)(2,1)}, u32[]{:S(2)}) copy-start(bf16[1,4,2,128,128]{4,3,2,1,0:T(8,128)(2,1)} %get-tuple-element.5) | copy-start | bytes 786436

commit v4 on v2

--- a/solution.py
+++ b/solution.py
@@ -49,9 +49,9 @@
 def kernel(
     steps, sites, parts, phys, owned,
     lc, rc, cs, cb, lseed, rseed, src, onsite, shift,
-    left_new, right_new,
-    hold_l, lrecv, lsend, rrecv, psend, terms, lct, site, bond, ys, zs, env_r, env_n,
-    gsend, grecv, usend, urecv, fsend, frecv, fall, tns, tnr, trs, trr,
+    site, fac, fall,
+    hold_l, lrecv, lsend, rrecv, psend, terms, lct, bond, ys, zs, env_r, env_n,
+    gsend, grecv, usend, urecv, fsend, frecv, tns, tnr, trs, trr,
     s_ls, s_lr, s_ps, s_pr, s_gs, s_gr, s_us, s_ur, s_fs, s_fr, s_tns, s_tnr, s_trs, s_trr,
 ):
     j = lax.axis_index("site")
@@ -292,12 +292,11 @@
         [dot_tn(bond[k], bond[k]) for k in range(owned)]
         + [dot_tn(site[k], site[k]) for k in range(owned)]
     )
-    factors = []
     for k in range(owned):
         hi, lo = split(zs[k])
         unit_t = dot_nt(hi, bond[k]) + dot_nt(lo, bond[k])
         usend[k] = unit_t.astype(BF16)
-        factors.append(mm(split(zs[owned + k]), split(unit_t)).astype(BF16))
+        fac[k] = mm(split(zs[owned + k]), split(unit_t)).astype(BF16)
     c_unit().start()
 
     for d in range(1, parts):
@@ -317,10 +316,6 @@
     for d in range(1, parts):
         c_factor(d).start()
 
-    for k in range(owned):
-        whole = dot(site[k], factors[k]).astype(BF16)
-        for s in range(phys):
-            left_new[0, s, k] = whole[s * width : (s + 1) * width]
     for i in range(owned):
         fall[off + i] = fsend[i]
     for d in range(1, parts):
@@ -328,11 +323,6 @@
         got(frecv.at[a], s_fr.at[a])
         for i in range(owned):
             fall[a * owned + i] = frecv[a, i]
-    for k in range(owned):
-        for s in range(phys):
-            block = site[k, s * width : (s + 1) * width]
-            right_new[0, s, k] = dot(fall[sources[s][k]], block).astype(BF16)
-
     def drain(t, carry):
         for d in range(parts):
             c_left(t, d).wait_send()
@@ -346,6 +336,17 @@
         for c in (c_seed, c_tn, c_gram, c_factor):
             c(d).wait_send()
     c_unit().wait_send()
+
+
+def finish(phys, owned, site, fac, fall, src, left_new, right_new):
+    off = lax.axis_index("sec") * owned
+    width = fac.shape[-1]
+    for k in range(owned):
+        whole = dot(site[k], fac[k]).astype(BF16)
+        for s in range(phys):
+            part = slice(s * width, (s + 1) * width)
+            left_new[0, s, k] = whole[part]
+            right_new[0, s, k] = dot(fall[src[0, s, off + k]], site[k, part]).astype(BF16)
 
 
 def per_device(lc, rc, cs, cb, lseed, rseed, src, onsite, shift):
@@ -365,11 +366,15 @@
     in_vmem = pl.BlockSpec(memory_space=pltpu.VMEM)
     in_smem = pl.BlockSpec(memory_space=pltpu.SMEM)
     shape = jax.ShapeDtypeStruct(cs.shape, BF16)
-    return pl.pallas_call(
+    site, fac, fall = pl.pallas_call(
         functools.partial(kernel, steps, sites, parts, phys, owned),
-        out_shape=(shape, shape),
+        out_shape=(
+            jax.ShapeDtypeStruct((owned, phys * width, width), BF16),
+            jax.ShapeDtypeStruct((owned, width, width), BF16),
+            jax.ShapeDtypeStruct((sectors, width, width), BF16),
+        ),
         in_specs=[in_vmem] * 6 + [in_smem] * 3,
-        out_specs=(in_vmem, in_vmem),
+        out_specs=(in_vmem,) * 3,
         scratch_shapes=[
             vm(sectors, *block),
             vm(steps + 1, parts, owned, *block),
@@ -378,7 +383,6 @@
             vm(steps, parts, owned, *block),
             vm(phys * owned, *block, dtype=F32),
             vm(owned, width, phys * width),
-            vm(owned, phys * width, width),
             vm(owned, *block),
             vm(most, *block, dtype=F32),
             vm(most, *block, dtype=F32),
@@ -390,7 +394,6 @@
             vm(owned, *block),
             vm(owned, *block),
             vm(parts, owned, *block),
-            vm(sectors, *block),
             vm(8, width, dtype=F32),
             vm(parts, 8, width, dtype=F32),
             vm(8, width, dtype=F32),
@@ -404,9 +407,16 @@
             dma(parts), dma(parts),
         ],
         compiler_params=pltpu.CompilerParams(
-            collective_id=0, has_side_effects=True, vmem_limit_bytes=60 * 1024 * 1024
+            collective_id=0, has_side_effects=True, vmem_limit_bytes=32 * 1024 * 1024
         ),
     )(lc, rc, cs, cb, lseed, rseed, src, onsite, shift)
+    return pl.pallas_call(
+        functools.partial(finish, phys, owned),
+        out_shape=(shape, shape),
+        in_specs=[in_vmem] * 3 + [in_smem],
+        out_specs=(in_vmem, in_vmem),
+        compiler_params=pltpu.CompilerParams(vmem_limit_bytes=16 * 1024 * 1024),
+    )(site, fac, fall, src)
 
 
 def solution(mesh):

time: 49.7 us -> 53.8 us (1.082)
  local copies, waits for them, and re-layouts: 2.42 us -> 6.04 us
    unnamed x4 -> x16, local copies, waits for them, and re-layouts: 2.42 us -> 6.04 us
    pallas_call x0 -> x1, Pallas kernels: none -> 1.65 us  [per_device(): pl.pallas_call(functools.partial(finish, phys, owned), out_shape=(shape,...]
    pallas_call x1, Pallas kernels: 45.8 us -> 44.4 us  [per_device(): pl.pallas_call(functools.partial(kernel, steps, sites, parts, phys, owned...]
where the time goes in v4:
time: 53.8 us; the launch traced here: 53.4 us
  Pallas kernels  46 us (86%)
  local copies, waits for them, and re-layouts  6.04 us (11%)
  between operations  1.33 us (2%)
    pallas_call x1, Pallas kernels, per_device(): pl.pallas_call(functools.partial(kernel, steps, sites, parts, phys, owned...  44.4 us
    unnamed x16, local copies, waits for them, and re-layouts  6.04 us
    pallas_call x1, Pallas kernels, per_device(): pl.pallas_call(functools.partial(finish, phys, owned), out_shape=(shape,...  1.65 us

profile of v4, /device:TPU:0, one launch (start us, length us, event | category | flops | bytes accessed | tf_op | source)
XLA Modules:
  0.0 53.4 jit_solution(10563403680180505278)
XLA Ops:
  0.6 0.0 copy-start.7
  1.3 0.0 copy-done.7
  1.3 0.0 copy-start
  1.3 0.9 %copy-done = bf16[1,4,2,128,128]{4,3,2,1,0:T(8,128)(2,1)S(1)} copy-done((bf16[1,4,2,128,128]{4,3,2,1,0:T(8,128)(2,1)S(1)}, bf16[1,4,2,128,128]{4,3,2,1,0:T(8,128)(2,1)}, u32[]{:S(2)}) %copy-start) | copy-done | bytes 262168
  2.3 0.0 copy-start.1
  2.3 0.9 %copy-done.1 = bf16[1,4,2,128,128]{4,3,2,1,0:T(8,128)(2,1)S(1)} copy-done((bf16[1,4,2,128,128]{4,3,2,1,0:T(8,128)(2,1)S(1)}, bf16[1,4,2,128,128]{4,3,2,1,0:T(8,128)(2,1)}, u32[]{:S(2)}) %copy-start.1) | copy-done | bytes 262168
  3.2 0.0 copy-start.2
  3.2 0.9 %copy-done.2 = bf16[1,4,2,128,128]{4,3,2,1,0:T(8,128)(2,1)S(1)} copy-done((bf16[1,4,2,128,128]{4,3,2,1,0:T(8,128)(2,1)S(1)}, bf16[1,4,2,128,128]{4,3,2,1,0:T(8,128)(2,1)}, u32[]{:S(2)}) %copy-start.2) | copy-done | bytes 262168
  4.2 0.0 copy-start.3
  4.2 0.8 %copy-done.3 = bf16[1,2,128,128]{3,2,1,0:T(8,128)(2,1)S(1)} copy-done((bf16[1,2,128,128]{3,2,1,0:T(8,128)(2,1)S(1)}, bf16[1,2,128,128]{3,2,1,0:T(8,128)(2,1)}, u32[]{:S(2)}) %copy-start.3) | copy-done | bytes 65560
  5.0 0.0 copy-start.4
  5.0 0.8 %copy-done.4 = bf16[1,2,128,128]{3,2,1,0:T(8,128)(2,1)S(1)} copy-done((bf16[1,2,128,128]{3,2,1,0:T(8,128)(2,1)S(1)}, bf16[1,2,128,128]{3,2,1,0:T(8,128)(2,1)}, u32[]{:S(2)}) %copy-start.4) | copy-done | bytes 65560
  5.8 0.0 copy-start.5
  5.8 0.8 %copy-done.5 = bf16[1,2,128,128]{3,2,1,0:T(8,128)(2,1)S(1)} copy-done((bf16[1,2,128,128]{3,2,1,0:T(8,128)(2,1)S(1)}, bf16[1,2,128,128]{3,2,1,0:T(8,128)(2,1)}, u32[]{:S(2)}) %copy-start.5) | copy-done | bytes 65560
  6.7 0.0 copy-start.6
  6.7 0.7 %copy-done.6 = s32[1,4,4]{2,1,0:T(4,128)S(1)} copy-done((s32[1,4,4]{2,1,0:T(4,128)S(1)}, s32[1,4,4]{2,1,0:T(4,128)}, u32[]{:S(2)}) %copy-start.6) | copy-done | bytes 88
  7.4 44.4 %shard_map.104 = (bf16[2,512,128]{2,1,0:T(8,128)(2,1)S(1)}, bf16[2,128,128]{2,1,0:T(8,128)(2,1)S(1)}, bf16[4,128,128]{2,1,0:T(8,128)(2,1)S(1)}) custom-call(bf16[1,4,2,128,128]{4,3,2,1,0:T(8,128)(2,1)S(1)} %copy-done, bf16[1,4,2,128,128]{4,3,2,1,0:T(8,128)(2,1)S(1)} %copy-done.1, bf16[1,4,2,128,128]{4,3,2,1,0:T(8,128)(2,1)S(1)} %copy-done.2, ...), custom_call_target="tpu_custom_call" | custom-call | tf_op jit(solution)/shard_map/pallas_call | solution.py:369
  51.7 1.6 %shard_map.105 = (bf16[1,4,2,128,128]{4,3,2,1,0:T(8,128)(2,1)}, bf16[1,4,2,128,128]{4,3,2,1,0:T(8,128)(2,1)}) custom-call(bf16[2,512,128]{2,1,0:T(8,128)(2,1)S(1)} %get-tuple-element.5.site, bf16[2,128,128]{2,1,0:T(8,128)(2,1)S(1)} %get-tuple-element.6.fac, bf16[4,128,128]{2,1,0:T(8,128)(2,1)S(1)} %get-tuple-element.7.fall, s32[1,4,4]{2,1,0:T(4,128)S(1)} %copy-done.6), custom_call_target="tpu_custom_call" | custom-call | tf_op jit(solution)/shard_map/pallas_call | solution.py:413
Async XLA Ops:
  0.6 0.7 %copy-start.7 = (f32[1,4]{1,0:T(1,128)S(1)}, f32[1,4]{1,0:T(1,128)}, u32[]{:S(2)}) copy-start(f32[1,4]{1,0:T(1,128)} %onsite.1) | copy-start | bytes 52
  1.3 1.0 %copy-start = (bf16[1,4,2,128,128]{4,3,2,1,0:T(8,128)(2,1)S(1)}, bf16[1,4,2,128,128]{4,3,2,1,0:T(8,128)(2,1)}, u32[]{:S(2)}) copy-start(bf16[1,4,2,128,128]{4,3,2,1,0:T(8,128)(2,1)} %lc.1) | copy-start | bytes 786436
  2.3 0.9 %copy-start.1 = (bf16[1,4,2,128,128]{4,3,2,1,0:T(8,128)(2,1)S(1)}, bf16[1,4,2,128,128]{4,3,2,1,0:T(8,128)(2,1)}, u32[]{:S(2)}) copy-start(bf16[1,4,2,128,128]{4,3,2,1,0:T(8,128)(2,1)} %rc.1) | copy-start | bytes 786436
  3.2 0.9 %copy-start.2 = (bf16[1,4,2,128,128]{4,3,2,1,0:T(8,128)(2,1)S(1)}, bf16[1,4,2,128,128]{4,3,2,1,0:T(8,128)(2,1)}, u32[]{:S(2)}) copy-start(bf16[1,4,2,128,128]{4,3,2,1,0:T(8,128)(2,1)} %cs.1) | copy-start | bytes 786436
  4.2 0.8 %copy-start.3 = (bf16[1,2,128,128]{3,2,1,0:T(8,128)(2,1)S(1)}, bf16[1,2,128,128]{3,2,1,0:T(8,128)(2,1)}, u32[]{:S(2)}) copy-start(bf16[1,2,128,128]{3,2,1,0:T(8,128)(2,1)} %cb.1) | copy-start | bytes 196612
  5.0 0.8 %copy-start.4 = (bf16[1,2,128,128]{3,2,1,0:T(8,128)(2,1)S(1)}, bf16[1,2,128,128]{3,2,1,0:T(8,128)(2,1)}, u32[]{:S(2)}) copy-start(bf16[1,2,128,128]{3,2,1,0:T(8,128)(2,1)} %lseed.1) | copy-start | bytes 196612
  5.8 0.8 %copy-start.5 = (bf16[1,2,128,128]{3,2,1,0:T(8,128)(2,1)S(1)}, bf16[1,2,128,128]{3,2,1,0:T(8,128)(2,1)}, u32[]{:S(2)}) copy-start(bf16[1,2,128,128]{3,2,1,0:T(8,128)(2,1)} %rseed.1) | copy-start | bytes 196612
  6.7 0.7 %copy-start.6 = (s32[1,4,4]{2,1,0:T(4,128)S(1)}, s32[1,4,4]{2,1,0:T(4,128)}, u32[]{:S(2)}) copy-start(s32[1,4,4]{2,1,0:T(4,128)} %src.3) | copy-start | bytes 196
